TPU v7x, 128 devices: a whole 4x4x4 slice. The times are simulated.
128 devices in a mesh: dp: 8 (over z_hi, y), mp: 8 (over z_lo, x), outer: 2 (over core).
Axes of the slice: x: 4, y: 4, z: 4 (z_hi: 2, z_lo: 2; z = z_hi * 2 + z_lo), core: 2. Of those that a mesh axis runs over, the one named last changes fastest.
Arguments:
- activations: bfloat16 [32768, 8192], P(('dp', 'outer'), 'mp'), may hold values from -6 to 6
- act_scale: float32 [256, 64], P(('dp', 'outer'), 'mp'), may hold values from 0.25 to 4
- out_grads: bfloat16 [32768, 16384], P(('dp', 'outer'), 'mp'), may hold values from -6 to 6
- gradient_tile_scale: float32 [256, 128], P(('dp', 'outer'), 'mp'), may hold values from 0.25 to 4
- prior_input_factor: float32 [8, 1024, 1024], P('mp', ('dp', 'outer')), may hold values from -0.3 to 6, as said below
- g_factor: float32 [16, 1024, 1024], P('mp', ('dp', 'outer')), may hold values from -0.3 to 6, as said below
- weight_grad: bfloat16 [8192, 16384], P('mp', ('dp', 'outer')), may hold values from -6 to 6
- a_inverse: bfloat16 [8, 1024, 1024], P('mp', ('dp', 'outer')), as said below
- g_inverse: bfloat16 [16, 1024, 1024], P(('dp', 'outer'), 'mp'), as said below
Outputs:
- a_stat: float32 [8, 1024, 1024], P('mp', ('dp', 'outer'))
- g_stat: float32 [16, 1024, 1024], P('mp', ('dp', 'outer'))
- new_a_factor: float32 [8, 1024, 1024], P('mp', ('dp', 'outer'))
- new_g_factor: float32 [16, 1024, 1024], P('mp', ('dp', 'outer'))
- preconditioned: bfloat16 [8192, 16384], P('mp', ('dp', 'outer'))
Inputs may be any that keep to these rules, and one draw needn't show every extreme that they name: `a_inverse`: each block is the identity plus dense off-diagonal and diagonal entries of magnitude at most 1.5 / sqrt(1024). `g_inverse`: each block is the identity plus dense off-diagonal and diagonal entries of magnitude at most 1.5 / sqrt(1024). `prior_input_factor`: each block is symmetric with a positive diagonal. `g_factor`: each block is symmetric with a positive diagonal.
All inputs are finite; a program needn't handle non-finite values.
Results may differ from a plain program's by a relative error of at most 0.014.
Values may be sent and summed in bfloat16 or wider, within the bound.
A program may use at most 128 MiB of HBM per device.

v0:
```python
import jax
import jax.numpy as jnp
from jax import lax
from jax.sharding import PartitionSpec as P

BLK = 1024
QT = 128
EMA_DECAY = 0.95


def dequantize(quantized, tile_scale):
    row_total, column_total = quantized.shape
    tiles_with_scale = (
        quantized.reshape(row_total // QT, QT, column_total // QT, QT)
        * tile_scale[:, None, :, None]
    )
    return tiles_with_scale.reshape(row_total, column_total).astype(jnp.bfloat16)


def body(
    activations,
    act_scale,
    out_grads,
    gradient_tile_scale,
    prior_input_factor,
    g_factor,
    weight_grad,
    a_inverse,
    g_inverse,
):
    input_factor_tiles = dequantize(activations, act_scale).reshape(activations.shape[0], -1, BLK)
    gradient_factor_tiles = dequantize(out_grads, gradient_tile_scale).reshape(
        out_grads.shape[0], -1, BLK
    )
    input_count = input_factor_tiles.shape[1]
    activation_rows = jnp.einsum(
        "qym,qyx->myx", input_factor_tiles, input_factor_tiles, preferred_element_type=jnp.float32
    )
    gradient_rows = jnp.einsum(
        "qym,qyx->myx",
        gradient_factor_tiles,
        gradient_factor_tiles,
        preferred_element_type=jnp.float32,
    )
    summed = lax.psum_scatter(
        jnp.concatenate([activation_rows, gradient_rows], axis=1).astype(jnp.bfloat16),
        ("dp", "outer"),
        scatter_dimension=0,
        tiled=True,
    ).astype(jnp.float32)
    token_total = activations.shape[0] * lax.axis_size("dp") * lax.axis_size("outer")
    statistics = jnp.transpose(summed, (1, 0, 2)) / token_total
    a_stat = statistics[:input_count]
    g_stat = statistics[input_count:]
    new_a_factor = EMA_DECAY * prior_input_factor + (1.0 - EMA_DECAY) * a_stat
    new_g_factor = EMA_DECAY * g_factor + (1.0 - EMA_DECAY) * g_stat
    row_blocks = weight_grad.shape[0] // BLK
    column_blocks = weight_grad.shape[1] // BLK
    grad_blocks = weight_grad.reshape(row_blocks, BLK, column_blocks, BLK)
    right = jnp.einsum(
        "aigk,gkl->aigl",
        grad_blocks,
        lax.all_gather(g_inverse, "mp", axis=1, tiled=True),
        preferred_element_type=jnp.float32,
    ).astype(jnp.bfloat16)
    result = jnp.einsum(
        "aij,ajgl->aigl",
        lax.all_gather(a_inverse, ("dp", "outer"), axis=1, tiled=True),
        right,
        preferred_element_type=jnp.float32,
    ).astype(jnp.bfloat16)
    return (
        a_stat,
        g_stat,
        new_a_factor,
        new_g_factor,
        result.reshape(row_blocks * BLK, column_blocks * BLK),
    )


def solution(mesh):
    return jax.shard_map(
        body,
        mesh=mesh,
        in_specs=(
            P(("dp", "outer"), "mp"),
            P(("dp", "outer"), "mp"),
            P(("dp", "outer"), "mp"),
            P(("dp", "outer"), "mp"),
            P("mp", ("dp", "outer"), None),
            P("mp", ("dp", "outer"), None),
            P("mp", ("dp", "outer")),
            P("mp", ("dp", "outer"), None),
            P(("dp", "outer"), "mp", None),
        ),
        out_specs=(
            P("mp", ("dp", "outer"), None),
            P("mp", ("dp", "outer"), None),
            P("mp", ("dp", "outer"), None),
            P("mp", ("dp", "outer"), None),
            P("mp", ("dp", "outer")),
        ),
        check_vma=False,
    )
```

profile of v0, /device:TPU:0, one launch (start us, length us, event | category | flops | bytes accessed | tf_op | source)
XLA Modules:
  0.0 278.4 jit_solution(16005743546915442506)
XLA Ops:
  7.2 0.0 copy-start
  7.2 0.0 all-gather.3.cloned.1.call-start
  7.2 0.7 all-gather.3.cloned.1.call-update
  7.9 0.0 all-gather.5.cloned.1.call-start
  8.0 0.7 all-gather.5.cloned.1.call-update
  8.7 0.0 all-reduce.3.cloned.1.call-start
  8.7 0.8 copy.36
  9.5 0.6 mul.46
  10.1 0.0 copy-start.3
  10.1 9.6 %convert_bitcast_fusion.2 = bf16[1024,1,1024]{0,2,1:T(8,128)(2,1)S(1)} fusion(f32[256,8,8,128]{3,2,1,0:T(8,128)S(1)} %bitcast.55, bf16[2048,1024]{1,0:T(8,128)(2,1)} %param.9), kind=kOutput, calls=%fused_computation.17 | convolution fusion | flops 4302307328 | bytes 14680064 | tf_op jit(solution)/shard_map/qym,qyx->myx/dot_general | solution.py:36
  19.7 0.0 copy-done.3
  19.7 1.1 mul.49
  20.8 11.8 %fusion = bf16[2048,2048]{1,0:T(8,128)(2,1)} fusion(f32[256,8,16,128]{3,2,1,0:T(8,128)S(1)} %bitcast.54, bf16[2048,2048]{1,0:T(8,128)(2,1)} %param.11), kind=kLoop, calls=%fused_computation.1 | loop fusion | flops 12582912 | bytes 33554432 | tf_op jit(solution)/shard_map/convert_element_type | solution.py:17
  32.6 13.8 %convert_bitcast_fusion = bf16[1024,2,1024]{0,2,1:T(8,128)(2,1)S(1)} fusion(bf16[256,2,8,1024]{3,2,1,0:T(8,128)(2,1)} %bitcast.56), kind=kOutput, calls=%fused_computation.9 | convolution fusion | flops 8592031744 | bytes 12582912 | tf_op jit(solution)/shard_map/qym,qyx->myx/dot_general | solution.py:39
  46.4 3.2 %pad_maximum_fusion = bf16[1024,3,1024]{0,2,1:T(8,128)(2,1)} fusion(bf16[1024,2,1024]{0,2,1:T(8,128)(2,1)S(1)} %convert_bitcast_fusion, bf16[1024,1,1024]{0,2,1:T(8,128)(2,1)S(1)} %convert_bitcast_fusion.2), kind=kLoop, calls=%fused_computation.7 | loop fusion | flops 3145728 | bytes 12582912 | tf_op jit(solution)/shard_map/concatenate | solution.py:46
  49.6 14.4 %copy.39 = bf16[1024,3,1024]{2,1,0:T(4,128)(2,1)} copy(bf16[1024,3,1024]{0,2,1:T(8,128)(2,1)} %pad_maximum_fusion) | data formatting | bytes 12582912 | tf_op jit(solution)/shard_map/concatenate | solution.py:46
  64.0 0.0 copy-start.4
  64.0 0.0 all-reduce.3.cloned.1.call-update
  64.0 0.6 copy-done.4
  64.7 0.6 dynamic-slice
  65.9 0.0 all-gather.3.cloned.1.call-done
  65.9 37.5 %all-gather.5.cloned.1.call-done = bf16[1,1024,1024]{2,1,0:T(8,128)(2,1)} async-done(((bf16[1,64,1024]{2,1,0:T(8,128)(2,1)}), bf16[1,1024,1024]{2,1,0:T(8,128)(2,1)}) %all-gather.5.cloned.1.call-update) | async-done | bytes 2097168 | tf_op jit(solution)/shard_map/all_gather | solution.py:68
  103.5 0.0 copy-done
  103.5 8.1 %convert_bitcast_fusion.1 = bf16[1024,1024]{0,1:T(8,128)(2,1)} fusion(bf16[1,1024,1024]{2,1,0:T(8,128)(2,1)} %all-gather.5.cloned.1.call-done, bf16[1024,1024]{1,0:T(8,128)(2,1)S(1)} %copy-done, bf16[1,1024,1024]{2,1,0:T(8,128)(2,1)} %all-gather.3.cloned.1.call-done), kind=kOutput, calls=%fused_computation.15 | convolution fusion | flops 4297064448 | bytes 8388608 | tf_op jit(solution)/shard_map/aij,ajgl->aigl/dot_general | solution.py:66
  111.6 4.0 %copy.41 = bf16[1024,1024]{1,0:T(8,128)(2,1)} copy(bf16[1024,1024]{0,1:T(8,128)(2,1)} %convert_bitcast_fusion.1) | data formatting | bytes 4194304
  115.6 152.9 %all-reduce.3.cloned.1.call-done = bf16[1024,3,1024]{2,1,0:T(4,128)(2,1)} async-done(((bf16[1024,3,1024]{2,1,0:T(4,128)(2,1)}), bf16[1024,3,1024]{2,1,0:T(4,128)(2,1)}) %all-reduce.3.cloned.1.call-update) | async-done | bytes 6291472
  268.5 1.2 constant_dynamic-slice_fusion
  269.7 0.2 multiply_bitcast_fusion
  269.9 0.0 copy-done.1
  269.9 1.1 multiply_add_fusion
  271.0 0.0 copy-done.2
  271.0 0.8 multiply_add_fusion.1
  (2 shorter events, 0.0 us)
Async XLA Ops:
  7.2 96.3 %copy-start = (bf16[1024,1024]{1,0:T(8,128)(2,1)S(1)}, bf16[1024,1024]{1,0:T(8,128)(2,1)}, u32[]{:S(2)}) copy-start(bf16[1024,1024]{1,0:T(8,128)(2,1)} %param.15) | copy-start | bytes 6291460
  7.2 58.7 %all-gather.3.cloned.1.call-start = ((), (), s32[]{:S(2)}) async-start(), calls=%async_computation | async-start | bytes 2359296 | tf_op jit(solution)/shard_map/all_gather | solution.py:63
  7.9 95.6 %all-gather.5.cloned.1.call-start = ((), (), s32[]{:S(2)}) async-start(), calls=%async_computation.1 | async-start | bytes 2228224 | tf_op jit(solution)/shard_map/all_gather | solution.py:68
  8.7 259.8 %all-reduce.3.cloned.1.call-start = ((), (), s32[]{:S(2)}) async-start(), calls=%async_computation.2 | async-start | bytes 16777216
  10.1 9.6 %copy-start.3 = (f32[16,16]{1,0:T(8,128)S(1)}, f32[16,16]{1,0:T(8,128)}, u32[]{:S(2)}) copy-start(f32[16,16]{1,0:T(8,128)} %param.12) | copy-start | bytes 3076
  64.0 0.7 copy-start.4
  111.6 158.4 %copy-start.1 = (f32[2,64,1024]{2,1,0:T(8,128)S(1)}, f32[2,64,1024]{2,1,0:T(8,128)}, u32[]{:S(2)}) copy-start(f32[2,64,1024]{2,1,0:T(8,128)} %param.14) | copy-start | bytes 1572868
  111.6 159.5 %copy-start.2 = (f32[1,64,1024]{2,1,0:T(8,128)S(1)}, f32[1,64,1024]{2,1,0:T(8,128)}, u32[]{:S(2)}) copy-start(f32[1,64,1024]{2,1,0:T(8,128)} %param.13) | copy-start | bytes 786436
Sparse Core Ops, SparseCore 0:
  9.6 43.7 all-gather.2
  55.8 47.5 all-gather.4
  106.0 162.4 all-reduce.2
where the time goes:
time: 279 us; the launch traced here: 278 us
  waiting for transfers between devices  192 us (69%)
  matrix products  31.4 us (11%)
  local copies, waits for them, and re-layouts  23.4 us (8%)
  other arithmetic  17.1 us (6%)
  between operations  14.5 us (5%)
    unnamed x4, waiting for transfers between devices  154 us
    all_gather x1, waiting for transfers between devices, body(): lax.all_gather(a_inverse, ('dp', 'outer'), axis=1, tiled=True)  37.5 us
    concatenate x1, local copies, waits for them, and re-layouts, body(): jnp.concatenate([activation_rows, gradient_rows], axis=1)  14.4 us
    dot_general x1, matrix products, body(): jnp.einsum('qym,qyx->myx', gradient_factor_tiles, gradient_factor_tiles,...  13.8 us
    convert_element_type x1, other arithmetic, dequantize(): tiles_with_scale.reshape(row_total, column_total).astype(jnp.bfloat16)  11.8 us
    dot_general x1, matrix products, body(): jnp.einsum('qym,qyx->myx', input_factor_tiles, input_factor_tiles, prefer...  9.56 us
    dot_general x1, matrix products, body(): jnp.einsum('aij,ajgl->aigl', lax.all_gather(a_inverse, ('dp', 'outer'), a...  8.1 us
    unnamed x14, local copies, waits for them, and re-layouts  7.24 us
  transfers between devices with their start and end apart: 3, of which 2 were waited for; matrix products, arithmetic and copies ran while one was open for 24% of the time, Pallas kernels for 0%

commit v1 on v0

--- a/solution.py
+++ b/solution.py
@@ -6,6 +6,13 @@
 BLK = 1024
 QT = 128
 EMA_DECAY = 0.95
+
+
+def gather_over(array, axis, d):
+    n_dev = lax.axis_size(axis)
+    parts = jnp.stack([array for _ in range(n_dev)])
+    parts = lax.all_to_all(parts, axis, split_axis=0, concat_axis=0)
+    return jnp.concatenate(parts, axis=d)
 
 
 def dequantize(quantized, tile_scale):
@@ -65,7 +72,7 @@
     ).astype(jnp.bfloat16)
     result = jnp.einsum(
         "aij,ajgl->aigl",
-        lax.all_gather(a_inverse, ("dp", "outer"), axis=1, tiled=True),
+        gather_over(a_inverse, ("dp", "outer"), 1),
         right,
         preferred_element_type=jnp.float32,
     ).astype(jnp.bfloat16)

time: 279 us -> 264 us (0.946)
  waiting for transfers between devices: 192 us -> 165 us
  starting transfers between devices: 0.11 us -> 8.14 us
    all_gather x1 -> x0, waiting for transfers between devices: 37.5 us -> none  [body(): lax.all_gather(a_inverse, ('dp', 'outer'), axis=1, tiled=True)]
    all_to_all x0 -> x1, waiting for transfers between devices: none -> 36.3 us  [gather_over(): parts = lax.all_to_all(parts, axis, split_axis=0, concat_axis=0)]
    unnamed x4 -> x3, waiting for transfers between devices: 154 us -> 129 us
    all_to_all x0 -> x1, starting transfers between devices: none -> 8.06 us  [gather_over(): parts = lax.all_to_all(parts, axis, split_axis=0, concat_axis=0)]
    unnamed x14 -> x16, local copies, waits for them, and re-layouts: 7.24 us -> 7.48 us
  transfers between devices with their start and end apart: 3 -> 3, of which waited for: 2 -> 2; matrix products, arithmetic and copies ran while one was open for 24% -> 26% of each run, Pallas kernels for 0% -> 0%
where the time goes in v1:
time: 264 us
  waiting for transfers between devices  165 us (62%)
  matrix products  31.5 us (12%)
  local copies, waits for them, and re-layouts  25.2 us (10%)
  other arithmetic  17.2 us (7%)
  between operations  16.2 us (6%)
  starting transfers between devices  8.14 us (3%)
    unnamed x3, waiting for transfers between devices  129 us
    all_to_all x1, waiting for transfers between devices, gather_over(): parts = lax.all_to_all(parts, axis, split_axis=0, concat_axis=0)  36.3 us
    concatenate x1, local copies, waits for them, and re-layouts, body(): jnp.concatenate([activation_rows, gradient_rows], axis=1)  14.4 us
    dot_general x1, matrix products, body(): jnp.einsum('qym,qyx->myx', gradient_factor_tiles, gradient_factor_tiles,...  13.8 us
    convert_element_type x1, other arithmetic, dequantize(): tiles_with_scale.reshape(row_total, column_total).astype(jnp.bfloat16)  11.8 us
    dot_general x1, matrix products, body(): jnp.einsum('qym,qyx->myx', input_factor_tiles, input_factor_tiles, prefer...  9.56 us
    dot_general x1, matrix products, body(): jnp.einsum('aij,ajgl->aigl', gather_over(a_inverse, ('dp', 'outer'), 1),...  8.19 us
    all_to_all x1, starting transfers between devices, gather_over(): parts = lax.all_to_all(parts, axis, split_axis=0, concat_axis=0)  8.06 us
  transfers between devices with their start and end apart: 3, of which 2 were waited for; matrix products, arithmetic and copies ran while one was open for 26% of the time, Pallas kernels for 0%

profile of v1, /device:TPU:0, one launch (start us, length us, event | category | flops | bytes accessed | tf_op | source)
XLA Modules:
  0.0 263.7 jit_solution(4347682718428510238)
XLA Ops:
  8.0 0.0 copy-start
  8.0 0.0 all-gather.2.cloned.1.call-start
  8.1 0.7 all-gather.2.cloned.1.call-update
  8.7 0.0 all-reduce.3.cloned.1.call-start
  8.8 0.8 copy.36
  9.6 0.6 mul.46
  10.2 0.0 copy-start.4
  10.2 9.6 %convert_bitcast_fusion.2 = bf16[1024,1,1024]{0,2,1:T(8,128)(2,1)S(1)} fusion(f32[256,8,8,128]{3,2,1,0:T(8,128)S(1)} %bitcast.53, bf16[2048,1024]{1,0:T(8,128)(2,1)} %param.9), kind=kOutput, calls=%fused_computation.16 | convolution fusion | flops 4302307328 | bytes 14680064 | tf_op jit(solution)/shard_map/qym,qyx->myx/dot_general | solution.py:43
  19.7 0.0 copy-done.4
  19.8 1.1 mul.49
  20.9 11.8 %fusion = bf16[2048,2048]{1,0:T(8,128)(2,1)} fusion(f32[256,8,16,128]{3,2,1,0:T(8,128)S(1)} %bitcast.52, bf16[2048,2048]{1,0:T(8,128)(2,1)} %param.11), kind=kLoop, calls=%fused_computation.1 | loop fusion | flops 12582912 | bytes 33554432 | tf_op jit(solution)/shard_map/convert_element_type | solution.py:24
  32.7 13.8 %convert_bitcast_fusion = bf16[1024,2,1024]{0,2,1:T(8,128)(2,1)S(1)} fusion(bf16[256,2,8,1024]{3,2,1,0:T(8,128)(2,1)} %bitcast.54), kind=kOutput, calls=%fused_computation.9 | convolution fusion | flops 8592031744 | bytes 12582912 | tf_op jit(solution)/shard_map/qym,qyx->myx/dot_general | solution.py:46
  46.5 3.2 %pad_maximum_fusion = bf16[1024,3,1024]{0,2,1:T(8,128)(2,1)} fusion(bf16[1024,2,1024]{0,2,1:T(8,128)(2,1)S(1)} %convert_bitcast_fusion, bf16[1024,1,1024]{0,2,1:T(8,128)(2,1)S(1)} %convert_bitcast_fusion.2), kind=kLoop, calls=%fused_computation.7 | loop fusion | flops 3145728 | bytes 12582912 | tf_op jit(solution)/shard_map/concatenate | solution.py:53
  49.7 14.4 %copy.39 = bf16[1024,3,1024]{2,1,0:T(4,128)(2,1)} copy(bf16[1024,3,1024]{0,2,1:T(8,128)(2,1)} %pad_maximum_fusion) | data formatting | bytes 12582912 | tf_op jit(solution)/shard_map/concatenate | solution.py:53
  64.1 0.0 all-reduce.3.cloned.1.call-update
  64.1 0.0 copy-start.5
  64.2 0.9 copy-done.3
  65.0 1.6 stack.2
  66.6 8.1 %all-to-all-start = ((bf16[16,1,64,1024]{3,2,1,0:T(8,128)(2,1)}), bf16[16,1,64,1024]{3,2,1,0:T(8,128)(2,1)}, u32[]{:S(2)}, u32[]{:S(2)}) async-start(bf16[16,1,64,1024]{3,2,1,0:T(8,128)(2,1)} %stack.2), calls=%async_computation | async-start | bytes 4194304 | tf_op jit(solution)/shard_map/all_to_all | solution.py:14
  74.7 0.0 copy-done.5
  74.7 0.6 dynamic-slice
  75.9 36.3 %all-to-all-done = bf16[16,1,64,1024]{3,2,1,0:T(8,128)(2,1)} async-done(((bf16[16,1,64,1024]{3,2,1,0:T(8,128)(2,1)}), bf16[16,1,64,1024]{3,2,1,0:T(8,128)(2,1)}, u32[]{:S(2)}, u32[]{:S(2)}) %all-to-all-start) | async-done | bytes 2097184 | tf_op jit(solution)/shard_map/all_to_all | solution.py:14
  112.2 0.0 copy-done
  112.2 8.2 %convert_bitcast_fusion.1 = bf16[1024,1024]{0,1:T(8,128)(2,1)} fusion(bf16[1024,1024]{1,0:T(8,128)(2,1)} %bitcast.9, bf16[1024,1024]{1,0:T(8,128)(2,1)S(1)} %copy-done, bf16[1,1024,1024]{2,1,0:T(8,128)(2,1)} %all-gather.2.cloned.1.call-done), kind=kOutput, calls=%fused_computation.14 | convolution fusion | flops 4297064448 | bytes 8388608 | tf_op jit(solution)/shard_map/aij,ajgl->aigl/dot_general | solution.py:73
  120.4 4.0 %copy.41 = bf16[1024,1024]{1,0:T(8,128)(2,1)} copy(bf16[1024,1024]{0,1:T(8,128)(2,1)} %convert_bitcast_fusion.1) | data formatting | bytes 4194304
  124.4 128.5 %all-reduce.3.cloned.1.call-done = bf16[1024,3,1024]{2,1,0:T(4,128)(2,1)} async-done(((bf16[1024,3,1024]{2,1,0:T(4,128)(2,1)}), bf16[1024,3,1024]{2,1,0:T(4,128)(2,1)}) %all-reduce.3.cloned.1.call-update) | async-done | bytes 6291472
  252.9 1.2 constant_dynamic-slice_fusion
  254.1 0.2 multiply_bitcast_fusion
  254.3 0.0 copy-done.1
  254.3 1.1 multiply_add_fusion
  255.4 0.0 copy-done.2
  255.4 0.8 multiply_add_fusion.1
  (4 shorter events, 0.0 us)
Async XLA Ops:
  8.0 104.2 %copy-start = (bf16[1024,1024]{1,0:T(8,128)(2,1)S(1)}, bf16[1024,1024]{1,0:T(8,128)(2,1)}, u32[]{:S(2)}) copy-start(bf16[1024,1024]{1,0:T(8,128)(2,1)} %param.15) | copy-start | bytes 6291460
  8.0 104.2 %all-gather.2.cloned.1.call-start = ((), (), s32[]{:S(2)}) async-start(), calls=%async_computation.1 | async-start | bytes 2359296 | tf_op jit(solution)/shard_map/all_gather | solution.py:70
  8.7 244.1 %all-reduce.3.cloned.1.call-start = ((), (), s32[]{:S(2)}) async-start(), calls=%async_computation.2 | async-start | bytes 16777216
  10.2 9.6 %copy-start.4 = (f32[16,16]{1,0:T(8,128)S(1)}, f32[16,16]{1,0:T(8,128)}, u32[]{:S(2)}) copy-start(f32[16,16]{1,0:T(8,128)} %param.12) | copy-start | bytes 3076
  64.1 0.9 copy-start.3
  64.1 10.5 %copy-start.5 = (u32[128]{0:T(128)S(1)}, u32[128]{0:T(128)}, u32[]{:S(2)}) copy-start(u32[128]{0:T(128)} %constant.15) | copy-start | bytes 1540
  66.6 45.6 %all-to-all-start = ((bf16[16,1,64,1024]{3,2,1,0:T(8,128)(2,1)}), bf16[16,1,64,1024]{3,2,1,0:T(8,128)(2,1)}, u32[]{:S(2)}, u32[]{:S(2)}) async-start(bf16[16,1,64,1024]{3,2,1,0:T(8,128)(2,1)} %stack.2), calls=%async_computation | async-start | bytes 4194304 | tf_op jit(solution)/shard_map/all_to_all | solution.py:14
  120.4 133.9 %copy-start.1 = (f32[2,64,1024]{2,1,0:T(8,128)S(1)}, f32[2,64,1024]{2,1,0:T(8,128)}, u32[]{:S(2)}) copy-start(f32[2,64,1024]{2,1,0:T(8,128)} %param.14) | copy-start | bytes 1572868
  120.4 135.0 %copy-start.2 = (f32[1,64,1024]{2,1,0:T(8,128)S(1)}, f32[1,64,1024]{2,1,0:T(8,128)}, u32[]{:S(2)}) copy-start(f32[1,64,1024]{2,1,0:T(8,128)} %param.13) | copy-start | bytes 786436
Sparse Core Ops, SparseCore 0:
  10.5 43.7 all-gather.1
Sparse Core Ops, SparseCore 1:
  64.2 188.6 all-reduce.2
